TPU v7x, 32 devices: a whole 2x2x4 slice. The times are simulated.
32 devices in a mesh: ctx: 16 (over z, y, x), grp: 2 (over core).
Axes of the slice: x: 2, y: 2, z: 4, core: 2. Of those that a mesh axis runs over, the one named last changes fastest.
Arguments:
- head_inputs: bfloat16 [32768, 80, 64], P('ctx', 'grp'), may hold values from -6 to 6
- gate_inputs: bfloat16 [32768, 80, 64], P('ctx', 'grp'), may hold values from -6 to 6
- step_raw: float32 [32768, 80], P('ctx', 'grp'), may hold values from -4 to 4
- step_bias: float32 [80], P('grp'), may hold values from -4 to -1
- decay_rate: float32 [80], P('grp'), may hold values from 3.0517578e-05 to 0.03125
- input_proj: bfloat16 [32768, 128], P('ctx'), may hold values from -6 to 6
- output_proj: bfloat16 [32768, 128], P('ctx'), may hold values from -6 to 6
- norm_gain: float32 [80, 64], P('grp'), may hold values from 0.5 to 1.5
Outputs:
- layer_out: bfloat16 [32768, 80, 64], P('ctx', 'grp')
All inputs are finite; a program needn't handle non-finite values.
Results may differ from a plain program's by a relative error of at most 0.001.
Values sent between devices are 32-bit elements.
A program may use at most 192 MiB of HBM per device.

v0:
```python
import jax
import jax.numpy as jnp
from jax import lax
from jax.sharding import PartitionSpec as P

HEADS = 80
HEAD_DIM = 64
BLOCK = 256


epsilon = 1e-05


def carried_in(shard, axis, combine, identity, reverse):
    count, position = lax.axis_size(axis), lax.axis_index(axis)
    everything = jax.tree.map(lambda part: lax.all_gather(part, axis), shard)
    start = jax.tree.map(
        lambda part, zero: jnp.broadcast_to(jnp.asarray(zero, part.dtype), part.shape),
        shard,
        identity,
    )

    def turn(k, before):
        at = count - 1 - k if reverse else k
        reached = at > position if reverse else at < position
        new = combine(before, jax.tree.map(lambda part: part[at], everything))
        return jax.tree.map(lambda a, b: jnp.where(reached, a, b), new, before)

    return lax.fori_loop(0, count, turn, start)


def block_within(scaled, decay_block, proj_in, proj_out):
    running = jnp.cumsum(decay_block, axis=0)
    length = decay_block.shape[0]
    causal = jnp.tril(jnp.ones((length, length), jnp.bool_))
    spread = running[:, None, :] - running[None, :, :]
    weights = jnp.exp(jnp.where(causal[:, :, None], spread, -jnp.inf))
    scores = jnp.dot(proj_out, proj_in.T, preferred_element_type=jnp.float32)
    within = jnp.einsum(
        "tsh,shp->thp", scores[:, :, None] * weights, scaled, precision=lax.Precision.HIGHEST
    )
    return (running, within)


def block_state(scaled, running, proj_in):
    remain = jnp.exp(running[-1][None, :] - running)
    return jnp.einsum(
        "shp,sn->hpn",
        scaled * remain[:, :, None],
        proj_in.astype(jnp.float32),
        precision=lax.Precision.HIGHEST,
    )


def read_out(proj_out, current):
    return jnp.einsum(
        "tn,hpn->thp", proj_out.astype(jnp.float32), current, precision=lax.Precision.HIGHEST
    )


def combine(earlier, later):
    return (earlier[0] * later[0], later[0][:, None, None] * earlier[1] + later[1])


def carry_in(decay_total, local_state):
    identity = (jnp.ones_like(decay_total), jnp.zeros_like(local_state))
    arrived = carried_in((decay_total, local_state), "ctx", combine, identity, False)
    incoming = arrived[1]
    return incoming


def shards(
    head_inputs, gate_inputs, step_raw, step_bias, decay_rate, input_proj, output_proj, norm_gain
):
    tok_rows, head_count, head_width = head_inputs.shape
    state_dim = input_proj.shape[1]
    blocks = tok_rows // BLOCK
    step_size = jax.nn.softplus(step_raw + step_bias)
    log_decay = -decay_rate * step_size
    raw_blocks = head_inputs.reshape(blocks, BLOCK, head_count, head_width)
    step_blocks = step_size.reshape(blocks, BLOCK, head_count)
    decay_blocks = log_decay.reshape(blocks, BLOCK, head_count)
    in_blocks = input_proj.reshape(blocks, BLOCK, state_dim)
    out_blocks = output_proj.reshape(blocks, BLOCK, state_dim)
    zero_state = jnp.zeros((head_count, head_width, state_dim), jnp.float32)
    zero_log = jnp.zeros((head_count,), jnp.float32)

    def advance(carried, block_in):
        current, offset = carried
        raw_block, step_block, decay_block, proj_in, proj_out = block_in
        scaled = raw_block.astype(jnp.float32) * step_block[:, :, None]
        running, within = block_within(scaled, decay_block, proj_in, proj_out)
        across = jnp.exp(running)[:, :, None] * read_out(proj_out, current)
        contrib = block_state(scaled, running, proj_in)
        current = jnp.exp(running[-1])[:, None, None] * current + contrib
        return ((current, offset + running[-1]), (within + across, offset[None, :] + running))

    finals, produced = lax.scan(
        advance,
        (zero_state, zero_log),
        (raw_blocks, step_blocks, decay_blocks, in_blocks, out_blocks),
    )
    local_state, total_log = finals
    partial_value = produced[0].reshape(tok_rows, head_count, head_width)
    reach_log = produced[1].reshape(tok_rows, head_count)
    incoming = carry_in(jnp.exp(total_log), local_state)
    mixed_out = partial_value + jnp.exp(reach_log)[:, :, None] * read_out(output_proj, incoming)
    gated_out = mixed_out * jax.nn.silu(gate_inputs.astype(jnp.float32))
    local_sq = jnp.sum(gated_out * gated_out, axis=(1, 2))
    total_sq = lax.psum(local_sq, "grp")
    mean_sq = total_sq / (HEADS * HEAD_DIM)
    result = gated_out * lax.rsqrt(mean_sq + epsilon)[:, None, None] * norm_gain
    return result.astype(jnp.bfloat16)


def solution(mesh):
    in_specs = (
        P("ctx", "grp", None),
        P("ctx", "grp", None),
        P("ctx", "grp"),
        P("grp"),
        P("grp"),
        P("ctx", None),
        P("ctx", None),
        P("grp", None),
    )
    out_specs = P("ctx", "grp", None)
    return jax.shard_map(shards, mesh=mesh, in_specs=in_specs, out_specs=out_specs, check_vma=False)
```

profile of v0, /device:TPU:25, one launch (start us, length us, event | category | flops | bytes accessed | tf_op | source)
XLA Modules:
  0.0 995.0 jit_solution(7291467283665147149)
XLA Ops:
  8.6 9.6 copy.59
  18.2 674.6 %while.31 = (s32[]{:T(128)}, f32[40,64,128]{2,1,0:T(8,128)}, f32[40]{0:T(128)S(1)}, f32[8,256,40,64]{1,0,3,2:T(8,128)}, f32[8,256,40]{1,2,0:T(8,128)}, /*index=5...) while((s32[]{:T(128)}, f32[40,64,128]{2,1,0:T(8,128)}, ...), condition=%wide.region_3.4_spmd.clone, body=%wide.region_0.3_spmd.clone.sunk | while | flops 4058489088 | bytes 26770636 | solution.py:98
  20.3 12.8 %fusion.80 = f32[40,64,256]{2,1,0:T(8,128)S(1)} fusion(f32[256,40]{0,1:T(8,128)S(1)} %bitcast_bitcast_fusion.2, f32[256,256]{1,0:T(8,128)S(1)} %fusion.79, pred[256,256]{1,0:T(8,128)(4,1)S(1)} %iota_compare_fusion.2, f32[256,40]{0,1:T(8,128)S(1)} %bitcast.151, bf16[8,256,40,64]{1,3,2,0:T(8,128)(2,1)} %get-tuple-element.419, s32[]{:T(128)S(6)} %copy.81), kind=kOutput, calls=%fused_computation.3.clone.1 | convolution fusion | flops 2022440960 | bytes 4382724 | tf_op jit(solution)/shard_map/while/body/eval_jaxpr/tsh,shp->thp/dot_general | solution.py:39
  33.4 2.1 fusion.81
  35.6 3.9 fusion.78
  39.5 2.7 copy.73
  42.2 58.8 %dynamic_update_slice.14 = f32[8,256,40,64]{1,0,3,2:T(8,128)} dynamic-update-slice(f32[8,256,40,64]{1,0,3,2:T(8,128)} %get-tuple-element.403, f32[1,256,40,64]{1,0,3,2:T(1,128)S(1)} %copy.73, s32[]{:T(128)S(6)} %copy.81, s32[]{:T(128)} %constant.65.clone.1..sunk, s32[]{:T(128)} %constant.65.clone.1..sunk, s32[]{:T(128)} %constant.65.clone.1..sunk) | dynamic-update-slice | bytes 5242884 | tf_op jit(solution)/shard_map/while/body/jit(dynamic_update_index_in_dim)/dynamic_update_slice | solution.py:98
  103.8 12.8 %fusion.80 = f32[40,64,256]{2,1,0:T(8,128)S(1)} fusion(f32[256,40]{0,1:T(8,128)S(1)} %bitcast_bitcast_fusion.2, f32[256,256]{1,0:T(8,128)S(1)} %fusion.79, pred[256,256]{1,0:T(8,128)(4,1)S(1)} %iota_compare_fusion.2, f32[256,40]{0,1:T(8,128)S(1)} %bitcast.151, bf16[8,256,40,64]{1,3,2,0:T(8,128)(2,1)} %get-tuple-element.419, s32[]{:T(128)S(6)} %copy.81), kind=kOutput, calls=%fused_computation.3.clone.1 | convolution fusion | flops 2022440960 | bytes 4382724 | tf_op jit(solution)/shard_map/while/body/eval_jaxpr/tsh,shp->thp/dot_general | solution.py:39
  116.9 2.6 fusion.81
  119.6 4.3 fusion.78
  124.0 2.7 copy.73
  126.7 58.8 %dynamic_update_slice.14 = f32[8,256,40,64]{1,0,3,2:T(8,128)} dynamic-update-slice(f32[8,256,40,64]{1,0,3,2:T(8,128)} %get-tuple-element.403, f32[1,256,40,64]{1,0,3,2:T(1,128)S(1)} %copy.73, s32[]{:T(128)S(6)} %copy.81, s32[]{:T(128)} %constant.65.clone.1..sunk, s32[]{:T(128)} %constant.65.clone.1..sunk, s32[]{:T(128)} %constant.65.clone.1..sunk) | dynamic-update-slice | bytes 5242884 | tf_op jit(solution)/shard_map/while/body/jit(dynamic_update_index_in_dim)/dynamic_update_slice | solution.py:98
  188.3 12.8 %fusion.80 = f32[40,64,256]{2,1,0:T(8,128)S(1)} fusion(f32[256,40]{0,1:T(8,128)S(1)} %bitcast_bitcast_fusion.2, f32[256,256]{1,0:T(8,128)S(1)} %fusion.79, pred[256,256]{1,0:T(8,128)(4,1)S(1)} %iota_compare_fusion.2, f32[256,40]{0,1:T(8,128)S(1)} %bitcast.151, bf16[8,256,40,64]{1,3,2,0:T(8,128)(2,1)} %get-tuple-element.419, s32[]{:T(128)S(6)} %copy.81), kind=kOutput, calls=%fused_computation.3.clone.1 | convolution fusion | flops 2022440960 | bytes 4382724 | tf_op jit(solution)/shard_map/while/body/eval_jaxpr/tsh,shp->thp/dot_general | solution.py:39
  201.4 2.6 fusion.81
  204.1 4.3 fusion.78
  208.4 2.7 copy.73
  211.1 58.8 %dynamic_update_slice.14 = f32[8,256,40,64]{1,0,3,2:T(8,128)} dynamic-update-slice(f32[8,256,40,64]{1,0,3,2:T(8,128)} %get-tuple-element.403, f32[1,256,40,64]{1,0,3,2:T(1,128)S(1)} %copy.73, s32[]{:T(128)S(6)} %copy.81, s32[]{:T(128)} %constant.65.clone.1..sunk, s32[]{:T(128)} %constant.65.clone.1..sunk, s32[]{:T(128)} %constant.65.clone.1..sunk) | dynamic-update-slice | bytes 5242884 | tf_op jit(solution)/shard_map/while/body/jit(dynamic_update_index_in_dim)/dynamic_update_slice | solution.py:98
  272.7 12.8 %fusion.80 = f32[40,64,256]{2,1,0:T(8,128)S(1)} fusion(f32[256,40]{0,1:T(8,128)S(1)} %bitcast_bitcast_fusion.2, f32[256,256]{1,0:T(8,128)S(1)} %fusion.79, pred[256,256]{1,0:T(8,128)(4,1)S(1)} %iota_compare_fusion.2, f32[256,40]{0,1:T(8,128)S(1)} %bitcast.151, bf16[8,256,40,64]{1,3,2,0:T(8,128)(2,1)} %get-tuple-element.419, s32[]{:T(128)S(6)} %copy.81), kind=kOutput, calls=%fused_computation.3.clone.1 | convolution fusion | flops 2022440960 | bytes 4382724 | tf_op jit(solution)/shard_map/while/body/eval_jaxpr/tsh,shp->thp/dot_general | solution.py:39
  285.8 2.6 fusion.81
  288.5 4.3 fusion.78
  292.8 2.7 copy.73
  295.5 58.8 %dynamic_update_slice.14 = f32[8,256,40,64]{1,0,3,2:T(8,128)} dynamic-update-slice(f32[8,256,40,64]{1,0,3,2:T(8,128)} %get-tuple-element.403, f32[1,256,40,64]{1,0,3,2:T(1,128)S(1)} %copy.73, s32[]{:T(128)S(6)} %copy.81, s32[]{:T(128)} %constant.65.clone.1..sunk, s32[]{:T(128)} %constant.65.clone.1..sunk, s32[]{:T(128)} %constant.65.clone.1..sunk) | dynamic-update-slice | bytes 5242884 | tf_op jit(solution)/shard_map/while/body/jit(dynamic_update_index_in_dim)/dynamic_update_slice | solution.py:98
  357.2 12.8 %fusion.80 = f32[40,64,256]{2,1,0:T(8,128)S(1)} fusion(f32[256,40]{0,1:T(8,128)S(1)} %bitcast_bitcast_fusion.2, f32[256,256]{1,0:T(8,128)S(1)} %fusion.79, pred[256,256]{1,0:T(8,128)(4,1)S(1)} %iota_compare_fusion.2, f32[256,40]{0,1:T(8,128)S(1)} %bitcast.151, bf16[8,256,40,64]{1,3,2,0:T(8,128)(2,1)} %get-tuple-element.419, s32[]{:T(128)S(6)} %copy.81), kind=kOutput, calls=%fused_computation.3.clone.1 | convolution fusion | flops 2022440960 | bytes 4382724 | tf_op jit(solution)/shard_map/while/body/eval_jaxpr/tsh,shp->thp/dot_general | solution.py:39
  370.3 2.6 fusion.81
  372.9 4.3 fusion.78
  377.3 2.7 copy.73
  380.0 58.8 %dynamic_update_slice.14 = f32[8,256,40,64]{1,0,3,2:T(8,128)} dynamic-update-slice(f32[8,256,40,64]{1,0,3,2:T(8,128)} %get-tuple-element.403, f32[1,256,40,64]{1,0,3,2:T(1,128)S(1)} %copy.73, s32[]{:T(128)S(6)} %copy.81, s32[]{:T(128)} %constant.65.clone.1..sunk, s32[]{:T(128)} %constant.65.clone.1..sunk, s32[]{:T(128)} %constant.65.clone.1..sunk) | dynamic-update-slice | bytes 5242884 | tf_op jit(solution)/shard_map/while/body/jit(dynamic_update_index_in_dim)/dynamic_update_slice | solution.py:98
  441.6 12.8 %fusion.80 = f32[40,64,256]{2,1,0:T(8,128)S(1)} fusion(f32[256,40]{0,1:T(8,128)S(1)} %bitcast_bitcast_fusion.2, f32[256,256]{1,0:T(8,128)S(1)} %fusion.79, pred[256,256]{1,0:T(8,128)(4,1)S(1)} %iota_compare_fusion.2, f32[256,40]{0,1:T(8,128)S(1)} %bitcast.151, bf16[8,256,40,64]{1,3,2,0:T(8,128)(2,1)} %get-tuple-element.419, s32[]{:T(128)S(6)} %copy.81), kind=kOutput, calls=%fused_computation.3.clone.1 | convolution fusion | flops 2022440960 | bytes 4382724 | tf_op jit(solution)/shard_map/while/body/eval_jaxpr/tsh,shp->thp/dot_general | solution.py:39
  454.7 2.6 fusion.81
  457.4 4.3 fusion.78
  461.7 2.7 copy.73
  464.4 58.8 %dynamic_update_slice.14 = f32[8,256,40,64]{1,0,3,2:T(8,128)} dynamic-update-slice(f32[8,256,40,64]{1,0,3,2:T(8,128)} %get-tuple-element.403, f32[1,256,40,64]{1,0,3,2:T(1,128)S(1)} %copy.73, s32[]{:T(128)S(6)} %copy.81, s32[]{:T(128)} %constant.65.clone.1..sunk, s32[]{:T(128)} %constant.65.clone.1..sunk, s32[]{:T(128)} %constant.65.clone.1..sunk) | dynamic-update-slice | bytes 5242884 | tf_op jit(solution)/shard_map/while/body/jit(dynamic_update_index_in_dim)/dynamic_update_slice | solution.py:98
  526.0 12.8 %fusion.80 = f32[40,64,256]{2,1,0:T(8,128)S(1)} fusion(f32[256,40]{0,1:T(8,128)S(1)} %bitcast_bitcast_fusion.2, f32[256,256]{1,0:T(8,128)S(1)} %fusion.79, pred[256,256]{1,0:T(8,128)(4,1)S(1)} %iota_compare_fusion.2, f32[256,40]{0,1:T(8,128)S(1)} %bitcast.151, bf16[8,256,40,64]{1,3,2,0:T(8,128)(2,1)} %get-tuple-element.419, s32[]{:T(128)S(6)} %copy.81), kind=kOutput, calls=%fused_computation.3.clone.1 | convolution fusion | flops 2022440960 | bytes 4382724 | tf_op jit(solution)/shard_map/while/body/eval_jaxpr/tsh,shp->thp/dot_general | solution.py:39
  539.1 2.6 fusion.81
  541.8 4.3 fusion.78
  546.2 2.7 copy.73
  548.8 58.8 %dynamic_update_slice.14 = f32[8,256,40,64]{1,0,3,2:T(8,128)} dynamic-update-slice(f32[8,256,40,64]{1,0,3,2:T(8,128)} %get-tuple-element.403, f32[1,256,40,64]{1,0,3,2:T(1,128)S(1)} %copy.73, s32[]{:T(128)S(6)} %copy.81, s32[]{:T(128)} %constant.65.clone.1..sunk, s32[]{:T(128)} %constant.65.clone.1..sunk, s32[]{:T(128)} %constant.65.clone.1..sunk) | dynamic-update-slice | bytes 5242884 | tf_op jit(solution)/shard_map/while/body/jit(dynamic_update_index_in_dim)/dynamic_update_slice | solution.py:98
  610.5 12.8 %fusion.80 = f32[40,64,256]{2,1,0:T(8,128)S(1)} fusion(f32[256,40]{0,1:T(8,128)S(1)} %bitcast_bitcast_fusion.2, f32[256,256]{1,0:T(8,128)S(1)} %fusion.79, pred[256,256]{1,0:T(8,128)(4,1)S(1)} %iota_compare_fusion.2, f32[256,40]{0,1:T(8,128)S(1)} %bitcast.151, bf16[8,256,40,64]{1,3,2,0:T(8,128)(2,1)} %get-tuple-element.419, s32[]{:T(128)S(6)} %copy.81), kind=kOutput, calls=%fused_computation.3.clone.1 | convolution fusion | flops 2022440960 | bytes 4382724 | tf_op jit(solution)/shard_map/while/body/eval_jaxpr/tsh,shp->thp/dot_general | solution.py:39
  623.6 2.6 fusion.81
  626.3 4.3 fusion.78
  630.6 2.7 copy.73
  633.3 58.8 %dynamic_update_slice.14 = f32[8,256,40,64]{1,0,3,2:T(8,128)} dynamic-update-slice(f32[8,256,40,64]{1,0,3,2:T(8,128)} %get-tuple-element.403, f32[1,256,40,64]{1,0,3,2:T(1,128)S(1)} %copy.73, s32[]{:T(128)S(6)} %copy.81, s32[]{:T(128)} %constant.65.clone.1..sunk, s32[]{:T(128)} %constant.65.clone.1..sunk, s32[]{:T(128)} %constant.65.clone.1..sunk) | dynamic-update-slice | bytes 5242884 | tf_op jit(solution)/shard_map/while/body/jit(dynamic_update_index_in_dim)/dynamic_update_slice | solution.py:98
  692.9 22.4 %reshape.68 = f32[2048,40,64]{0,2,1:T(8,128)} reshape(f32[8,256,40,64]{1,0,3,2:T(8,128)} %get-tuple-element.154) | data formatting | bytes 41943040 | tf_op jit(solution)/shard_map/reshape | solution.py:104
  716.7 27.2 %all-reduce = f32[640]{0:T(1024)S(1)} all-reduce(f32[640]{0:T(1024)S(1)} %exponential_dynamic-update-slice_fusion), channel_id=2, replica_groups=mesh['ctx'=16,'grp'=2] {'ctx'}, use_global_device_ids=true, to_apply=%add | all-reduce | flops 640 | bytes 5120
  744.1 178.6 %all-gather.4.cloned.1.call-done = f32[640,64,128]{2,1,0:T(8,128)} async-done(((f32[40,64,128]{2,1,0:T(8,128)}), f32[640,64,128]{2,1,0:T(8,128)}) %all-gather.4.cloned.1.call-update) | async-done | bytes 20971536 | tf_op jit(solution)/shard_map/all_gather | solution.py:16
  922.7 26.6 %while.32 = (s32[]{:T(128)}, f32[40,64,128]{2,1,0:T(8,128)S(1)}, s32[]{:T(128)}, f32[16,40]{1,0:T(8,128)S(1)}, f32[16,40,64,128]{3,2,1,0:T(8,128)}, /*index=5*/s32[]{:T(128)}, s32[]{:T(128)}) while((s32[]{:T(128)}, f32[40,64,128]{2,1,0:T(8,128)S(1)}, s32[]{:T(128)}, f32[16,40]{1,0:T(8,128)S(1)}, f32[16,40,64,128]{3,2,1,0:T(8,128)}, ...), condition=%wide.region_5.6_spmd.clone, body=%wide.region_4.5_spmd.clone.sunk | while | flops 1310724 | bytes 3932753 | solution.py:29
  924.3 1.6 fusion.82
  926.0 1.6 fusion.82
  927.7 1.6 fusion.82
  929.3 1.6 fusion.82
  931.0 1.6 fusion.82
  932.7 1.6 fusion.82
  934.3 1.6 fusion.82
  936.0 1.6 fusion.82
  937.6 1.6 fusion.82
  939.3 1.6 fusion.82
  941.0 1.6 fusion.82
  942.6 1.6 fusion.82
  944.3 1.6 fusion.82
  946.0 1.6 fusion.82
  947.6 1.6 fusion.82
  949.3 23.1 %multiply_reduce_fusion = (f32[2048]{0:T(1024)S(1)}, f32[2048,40,64]{0,2,1:T(8,128)}) fusion(bf16[2048,40,64]{0,2,1:T(8,128)(2,1)} %param.13, f32[2048,40,64]{0,2,1:T(8,128)} %reshape.68, f32[40,64,128]{2,1,0:T(8,128)S(1)} %get-tuple-element.158, bf16[2048,128]{1,0:T(8,128)(2,1)} %param.18, f32[2048,40]{0,1:T(8,128)S(1)} %bitcast.158), kind=kOutput, calls=%fused_computation.68 | convolution fusion | flops 8105490432 | bytes 54599680 | tf_op jit(solution)/shard_map/tn,hpn->thp/dot_general | solution.py:56
  972.4 3.2 psum.7
  975.6 12.5 %multiply_convert_fusion = bf16[2048,40,64]{0,2,1:T(8,128)(2,1)} fusion(f32[2048,40,64]{0,2,1:T(8,128)} %get-tuple-element.280, f32[40,64]{1,0:T(8,128)S(1)} %copy-done.1, f32[2048]{0:T(1024)S(1)} %add_rsqrt_fusion), kind=kLoop, calls=%fused_computation.67 | loop fusion | flops 15728640 | bytes 31475712 | tf_op jit(solution)/shard_map/convert_element_type | solution.py:113
  (153 shorter events, 29.1 us)
Async XLA Ops:
  6.5 916.1 %all-gather.4.cloned.1.call-start = ((), (), s32[]{:S(2)}) async-start(), calls=%async_computation | async-start | bytes 22282240 | tf_op jit(solution)/shard_map/all_gather | solution.py:16
  692.9 22.4 %copy-start.2 = (u32[32]{0:T(128)S(1)}, u32[32]{0:T(128)}, u32[]{:S(2)}) copy-start(u32[32]{0:T(128)} %constant.74) | copy-start | bytes 388
  692.9 51.1 %copy-start = (f32[8,256,40]{1,2,0:T(8,128)S(1)}, f32[8,256,40]{1,2,0:T(8,128)}, u32[]{:S(2)}) copy-start(f32[8,256,40]{1,2,0:T(8,128)} %get-tuple-element.155) | copy-start | bytes 983044
  949.2 26.4 %copy-start.1 = (f32[40,64]{1,0:T(8,128)S(1)}, f32[40,64]{1,0:T(8,128)}, u32[]{:S(2)}) copy-start(f32[40,64]{1,0:T(8,128)} %param.19) | copy-start | bytes 30724
Sparse Core Ops, SparseCore 0:
  693.0 229.6 all-gather.3
where the time goes:
time: 1010 us; the launch traced here: 995 us
  local copies, waits for them, and re-layouts  529 us (52%)
  matrix products  189 us (19%)
  waiting for transfers between devices  179 us (18%)
  other arithmetic  52.7 us (5%)
  blocking collectives  30.4 us (3%)
  between operations  14.2 us (1%)
    dynamic_update_slice x16, local copies, waits for them, and re-layouts, shards(): lax.scan(advance, (zero_state, zero_log), (raw_blocks, step_blocks, decay...  492 us
    all_gather x1, waiting for transfers between devices, carried_in(): everything = jax.tree.map(lambda part: lax.all_gather(part, axis), shard)  179 us
    dot_general x8, matrix products, block_within(): jnp.einsum('tsh,shp->thp', scores[:, :, None] * weights, scaled, precisio...  103 us
    dot_general x9, matrix products, read_out(): jnp.einsum('tn,hpn->thp', proj_out.astype(jnp.float32), current, precisio...  43.8 us
    dot_general x8, matrix products, block_state(): jnp.einsum('shp,sn->hpn', scaled * remain[:, :, None], proj_in.astype(jnp...  34.3 us
    unnamed x1, blocking collectives  27.2 us
    select_n x16, other arithmetic, turn(): return jax.tree.map(lambda a, b: jnp.where(reached, a, b), new, before)  25.9 us
    reshape x1, local copies, waits for them, and re-layouts, shards(): partial_value = produced[0].reshape(tok_rows, head_count, head_width)  22.4 us
  transfers between devices with their start and end apart: 1, of which 1 were waited for; matrix products, arithmetic and copies ran while one was open for 2% of the time, Pallas kernels for 0%

commit v1 on v0

v1 whole, which is shorter than its diff:
```python
import functools

import jax
import jax.numpy as jnp
from jax import lax
from jax.experimental import pallas as pl
from jax.experimental.pallas import tpu as pltpu
from jax.sharding import PartitionSpec as P

BLOCK = 256
EPS = 1e-05
NT = (((1,), (1,)), ((), ()))
F32, BF16 = jnp.float32, jnp.bfloat16


def dot(a, b):
    return jnp.dot(a, b, preferred_element_type=F32)


def split(v):
    hi = v.astype(BF16)
    return hi, (v - hi.astype(F32)).astype(BF16)


def decays(raw, bias, rate):
    v = raw + bias
    step = jnp.maximum(v, 0.0) + jnp.log1p(jnp.exp(-jnp.abs(v)))
    log = -rate * step
    q = raw.shape[1]
    upto = lax.broadcasted_iota(jnp.int32, (q, q), 0) <= lax.broadcasted_iota(jnp.int32, (q, q), 1)
    upto = upto.astype(BF16)
    a, rest = log.astype(BF16), log - log.astype(BF16).astype(F32)
    b, c = split(rest)
    running = dot(a, upto) + dot(b, upto) + dot(c, upto)
    return step, running


def scaled_rows(x_ref, w_ref, yhi_ref, ylo_ref, first, group, width):
    for i in range(group):
        h = first + i
        w = w_ref[pl.ds(h, 1), :]
        y = x_ref[pl.ds(pl.multiple_of(h * width, width), width), :].astype(F32) * w
        hi, lo = split(y)
        yhi_ref[i * width:(i + 1) * width, :] = hi
        ylo_ref[i * width:(i + 1) * width, :] = lo


def state_kernel(heads, width, group, x_ref, raw_ref, bias_ref, rate_ref, b_ref,
                 loc_ref, last_ref, log_ref, s_ref, w_ref, e_ref, t_ref, yhi_ref, ylo_ref):
    c = pl.program_id(0)

    @pl.when(c == 0)
    def _():
        s_ref[...] = jnp.zeros_like(s_ref)
        t_ref[...] = jnp.zeros_like(t_ref)

    step, running = decays(raw_ref[...], bias_ref[...], rate_ref[...])
    end = jnp.broadcast_to(running[:, -1:], e_ref.shape)
    w_ref[...] = step * jnp.exp(-running)
    e_ref[...] = jnp.exp(end)
    t_ref[...] += end
    rows = group * width

    def body(g, carry):
        first = g * group
        at = pl.ds(pl.multiple_of(first * width, width), rows)
        scaled_rows(x_ref, w_ref, yhi_ref, ylo_ref, first, group, width)
        part = dot(yhi_ref[...], b_ref[...]) + dot(ylo_ref[...], b_ref[...])
        old = s_ref[at, :]
        loc_ref[0, at, :] = old
        new = old + part
        for i in range(group):
            s_ref[pl.ds(pl.multiple_of((first + i) * width, width), width), :] = (
                new[i * width:(i + 1) * width, :] * e_ref[pl.ds(first + i, 1), :])
        return carry

    lax.fori_loop(0, heads // group, body, 0)
    last_ref[...] = s_ref[...]
    log_ref[...] = t_ref[...]


def output_kernel(heads, width, group, x_ref, gate_ref, raw_ref, bias_ref, rate_ref, b_ref, c_ref,
                  loc_ref, init_ref, out_ref, sq_ref,
                  w_ref, e_ref, t_ref, d_ref, yhi_ref, ylo_ref, shl_ref):
    c = pl.program_id(0)

    @pl.when(c == 0)
    def _():
        t_ref[...] = jnp.zeros_like(t_ref)

    step, running = decays(raw_ref[...], bias_ref[...], rate_ref[...])
    w_ref[...] = step * jnp.exp(-running)
    e_ref[...] = jnp.exp(running)
    d_ref[...] = jnp.exp(t_ref[...])
    t_ref[...] += jnp.broadcast_to(running[:, -1:], t_ref.shape)
    rows = group * width
    q, n = b_ref.shape
    scores = lax.dot_general(b_ref[...], c_ref[...], NT, preferred_element_type=F32)
    causal = lax.broadcasted_iota(jnp.int32, (q, q), 0) <= lax.broadcasted_iota(jnp.int32, (q, q), 1)
    mhi, mlo = split(jnp.where(causal, scores, 0.0))
    twice = jnp.concatenate([c_ref[...], c_ref[...]], axis=1)

    def body(g, total):
        first = g * group
        scaled_rows(x_ref, w_ref, yhi_ref, ylo_ref, first, group, width)
        for i in range(group):
            at = pl.ds(pl.multiple_of((first + i) * width, width), width)
            s = loc_ref[0, at, :] + init_ref[at, :] * d_ref[pl.ds(first + i, 1), :]
            hi, lo = split(s)
            shl_ref[i * width:(i + 1) * width, :n] = hi
            shl_ref[i * width:(i + 1) * width, n:] = lo
        mixed = (dot(yhi_ref[...], mhi) + dot(ylo_ref[...], mhi) + dot(yhi_ref[...], mlo)
                 + lax.dot_general(shl_ref[...], twice, NT, preferred_element_type=F32))
        for i in range(group):
            at = pl.ds(pl.multiple_of((first + i) * width, width), width)
            v = gate_ref[at, :].astype(F32)
            half = 0.5 * v
            silu = half + half * jnp.tanh(half)
            gated = mixed[i * width:(i + 1) * width, :] * e_ref[pl.ds(first + i, 1), :] * silu
            out_ref[at, :] = gated
            total = total + jnp.sum((gated * gated).reshape(width // 8, 8, q), axis=0)
        return total

    total = lax.fori_loop(0, heads // group, body, jnp.zeros((8, q), F32))
    sq_ref[...] = jnp.sum(total, axis=0, keepdims=True)


def group_of(heads, most=10):
    return max(k for k in range(1, most + 1) if heads % k == 0)


def carry(last, logs, width):
    count, here = lax.axis_size("ctx"), lax.axis_index("ctx")
    inner = 4 if count % 4 == 0 else 2 if count % 2 == 0 else 1
    outer = count // inner
    rows, n = last.shape
    heads = logs.shape[0]
    part = rows // inner
    me = here % inner
    parts = last.reshape(inner, part, n)
    wide = [jnp.concatenate([lax.dynamic_index_in_dim(parts, me ^ k, 0, False), logs], 0)
            for k in range(inner)]
    got = [wide[0]] + [
        lax.ppermute(wide[k], "ctx", [(i, i ^ k) for i in range(count)]) for k in range(1, inner)]
    got = jnp.stack(got)

    def spread(log):
        long = jnp.repeat(log, width, axis=0).reshape(inner, part, n)
        return lax.dynamic_index_in_dim(long, me, 0, False)

    before, prefix, since = jnp.zeros((part, n), F32), [], jnp.zeros((heads, n), F32)
    logs_before = []
    for k in range(inner):
        piece = lax.dynamic_index_in_dim(got, me ^ k, 0, False)
        prefix.append(before)
        logs_before.append(since)
        log = piece[part:]
        before = before * jnp.exp(spread(log)) + piece[:part]
        since = since + log
    total, total_log = before, since
    acc = lax.ppermute(jnp.concatenate([total, total_log], 0), "ctx",
                       [(i, i + inner) for i in range(count - inner)])
    shift = 1
    while shift < outer - 1:
        earlier = lax.ppermute(acc, "ctx", [(i, i + shift * inner) for i in range(count - shift * inner)])
        state = acc[:part] + jnp.exp(spread(acc[part:])) * earlier[:part]
        acc = jnp.concatenate([state, acc[part:] + earlier[part:]], 0)
        shift *= 2
    entering = acc[:part]
    finals = jnp.stack([p + jnp.exp(spread(l)) * entering for p, l in zip(prefix, logs_before)])
    mine = [lax.dynamic_index_in_dim(finals, me ^ k, 0, False) for k in range(inner)]
    back = [mine[0]] + [
        lax.ppermute(mine[k], "ctx", [(i, i ^ k) for i in range(count)]) for k in range(1, inner)]
    back = jnp.stack(back)
    return jnp.concatenate([lax.dynamic_index_in_dim(back, me ^ k, 0, False) for k in range(inner)], 0)


def shards(head_inputs, gate_inputs, step_raw, step_bias, decay_rate, input_proj, output_proj, norm_gain):
    tokens, heads, width = head_inputs.shape
    n = input_proj.shape[1]
    rows = heads * width
    blocks = tokens // BLOCK
    group = group_of(heads)
    x = jnp.transpose(head_inputs, (1, 2, 0)).reshape(rows, tokens)
    gate = jnp.transpose(gate_inputs, (1, 2, 0)).reshape(rows, tokens)
    raw = step_raw.T
    bias, rate = step_bias[:, None], decay_rate[:, None]

    wide = pl.BlockSpec((rows, BLOCK), lambda c: (0, c))
    per_head = pl.BlockSpec((heads, BLOCK), lambda c: (0, c))
    whole = lambda *shape: pl.BlockSpec(shape, lambda c: (0,) * len(shape))
    proj = pl.BlockSpec((BLOCK, n), lambda c: (c, 0))
    local = pl.BlockSpec((1, rows, n), lambda c: (c, 0, 0))
    params = pltpu.CompilerParams(dimension_semantics=("arbitrary",), vmem_limit_bytes=60 << 20)
    ys = [pltpu.VMEM((group * width, BLOCK), BF16)] * 2

    loc, last, logs = pl.pallas_call(
        functools.partial(state_kernel, heads, width, group),
        grid=(blocks,),
        in_specs=[wide, per_head, whole(heads, 1), whole(heads, 1), proj],
        out_specs=[local, whole(rows, n), whole(heads, n)],
        out_shape=[jax.ShapeDtypeStruct((blocks, rows, n), F32),
                   jax.ShapeDtypeStruct((rows, n), F32),
                   jax.ShapeDtypeStruct((heads, n), F32)],
        scratch_shapes=[pltpu.VMEM((rows, n), F32), pltpu.VMEM((heads, BLOCK), F32),
                        pltpu.VMEM((heads, n), F32), pltpu.VMEM((heads, n), F32)] + ys,
        compiler_params=params, name="local_state",
    )(x, raw, bias, rate, input_proj)

    init = carry(last, logs, width)

    gated, local_sq = pl.pallas_call(
        functools.partial(output_kernel, heads, width, group),
        grid=(blocks,),
        in_specs=[wide, wide, per_head, whole(heads, 1), whole(heads, 1), proj, proj, local, whole(rows, n)],
        out_specs=[wide, pl.BlockSpec((1, BLOCK), lambda c: (0, c))],
        out_shape=[jax.ShapeDtypeStruct((rows, tokens), F32), jax.ShapeDtypeStruct((1, tokens), F32)],
        scratch_shapes=[pltpu.VMEM((heads, BLOCK), F32), pltpu.VMEM((heads, BLOCK), F32),
                        pltpu.VMEM((heads, n), F32), pltpu.VMEM((heads, n), F32)] + ys
                       + [pltpu.VMEM((group * width, 2 * n), BF16)],
        compiler_params=params, name="outputs",
    )(x, gate, raw, bias, rate, input_proj, output_proj, loc, init)

    total_sq = lax.psum(local_sq, "grp")
    channels = lax.axis_size("grp") * rows
    scale = lax.rsqrt(total_sq / channels + EPS)
    result = (gated * scale * norm_gain.reshape(rows, 1)).astype(BF16)
    return jnp.transpose(result.reshape(heads, width, tokens), (2, 0, 1))


def solution(mesh):
    in_specs = (P("ctx", "grp", None), P("ctx", "grp", None), P("ctx", "grp"), P("grp"), P("grp"),
                P("ctx", None), P("ctx", None), P("grp", None))
    return jax.shard_map(shards, mesh=mesh, in_specs=in_specs, out_specs=P("ctx", "grp", None), check_vma=False)
```

time: 1010 us -> 143 us (0.14); the launches traced: 995 us -> 143 us
  local copies, waits for them, and re-layouts: 529 us -> 5.01 us
  matrix products: 189 us -> 0 us
  waiting for transfers between devices: 179 us -> 63.8 us
  Pallas kernels: 0 us -> 45.5 us
  other arithmetic: 52.7 us -> 15.2 us
  blocking collectives: 30.4 us -> 4.03 us
  between operations: 14.2 us -> 0.19 us
    dynamic_update_slice x16 -> x0, local copies, waits for them, and re-layouts: 492 us -> none  [shards(): lax.scan(advance, (zero_state, zero_log), (raw_blocks, step_blocks, decay...]
    dot_general x33 -> x0, matrix products: 189 us -> none  [the longest x8 103 us: block_within(): jnp.einsum('tsh,shp->thp', scores[:, :, None] * weights, scaled, precisio...]
    all_gather x1 -> x0, waiting for transfers between devices: 179 us -> none  [carried_in(): everything = jax.tree.map(lambda part: lax.all_gather(part, axis), shard)]
    ppermute x0 -> x9, waiting for transfers between devices: none -> 63.8 us  [the longest x2 26.4 us: carry(): lax.ppermute(acc, 'ctx', [(i, i + shift * inner) for i in range(count - s...]
    pallas_call x0 -> x2, Pallas kernels: none -> 45.5 us  [the longest x1 27.1 us: shards(): pl.pallas_call(functools.partial(output_kernel, heads, width, group), gri...]
    reshape x10 -> x0, local copies, waits for them, and re-layouts: 32 us -> none  [the longest x1 22.4 us: shards(): partial_value = produced[0].reshape(tok_rows, head_count, head_width)]
    unnamed x1 -> x0, blocking collectives: 27.2 us -> none
    select_n x16 -> x0, other arithmetic: 25.9 us -> none  [turn(): return jax.tree.map(lambda a, b: jnp.where(reached, a, b), new, before)]
  transfers between devices with their start and end apart: 1 -> 9, of which waited for: 1 -> 8; matrix products, arithmetic and copies ran while one was open for 2% -> 0% of each run, Pallas kernels for 0% -> 0%
where the time goes in v1:
time: 143 us
  waiting for transfers between devices  63.8 us (45%)
  Pallas kernels  45.5 us (32%)
  other arithmetic  15.2 us (11%)
  starting transfers between devices  9.38 us (7%)
  local copies, waits for them, and re-layouts  5.01 us (4%)
  blocking collectives  4.03 us (3%)
    pallas_call x1, Pallas kernels, shards(): pl.pallas_call(functools.partial(output_kernel, heads, width, group), gri...  27.1 us
    ppermute x2, waiting for transfers between devices, carry(): lax.ppermute(acc, 'ctx', [(i, i + shift * inner) for i in range(count - s...  26.4 us
    pallas_call x1, Pallas kernels, shards(): pl.pallas_call(functools.partial(state_kernel, heads, width, group), grid...  18.4 us
    ppermute x3, waiting for transfers between devices, carry(): lax.ppermute(wide[k], 'ctx', [(i, i ^ k) for i in range(count)])  14.8 us
    ppermute x3, waiting for transfers between devices, carry(): lax.ppermute(mine[k], 'ctx', [(i, i ^ k) for i in range(count)])  14.1 us
    convert_element_type x1, other arithmetic, shards(): result = (gated * scale * norm_gain.reshape(rows, 1)).astype(BF16)  12.8 us
    ppermute x1, waiting for transfers between devices, carry(): lax.ppermute(jnp.concatenate([total, total_log], 0), 'ctx', [(i, i + inne...  8.49 us
    psum x1, blocking collectives, shards(): total_sq = lax.psum(local_sq, 'grp')  4.03 us
  transfers between devices with their start and end apart: 9, of which 8 were waited for; matrix products, arithmetic and copies ran while one was open for 0% of the time, Pallas kernels for 0%

profile of v1, /device:TPU:25, one launch (start us, length us, event | category | flops | bytes accessed | tf_op | source)
XLA Modules:
  0.0 143.0 jit_solution(2666490690785531870)
XLA Ops:
  0.0 1.3 copy.11.bias_ref
  1.3 1.3 copy.12.rate_ref
  2.7 18.4 %local_state.1 = (f32[8,2560,128]{2,1,0:T(8,128)}, f32[2560,128]{1,0:T(8,128)}, f32[40,128]{1,0:T(8,128)}) custom-call(bf16[2560,2048]{1,0:T(8,128)(2,1)} %bitcast.145, f32[40,2048]{1,0:T(8,128)} %bitcast.159, f32[40,1]{1,0:T(8,128)} %copy.11.bias_ref, f32[40,1]{1,0:T(8,128)} %copy.12.rate_ref, bf16[2048,128]{1,0:T(8,128)(2,1)} %b_ref.3), custom_call_target="tpu_custom_call" | custom-call | tf_op jit(solution)/shard_map/local_state/pallas_call | solution.py:197
  21.1 0.0 copy-start
  21.1 1.4 dynamic-slice_bitcast_fusion.14
  22.5 0.0 copy-done
  22.5 0.1 fusion
  22.6 1.3 collective-permute-start
  23.9 1.3 collective-permute-start.1
  25.1 0.2 collective-permute-start.2
  25.3 6.4 %collective-permute-done = f32[680,128]{1,0:T(8,128)S(1)} collective-permute-done((f32[680,128]{1,0:T(8,128)S(1)}, f32[680,128]{1,0:T(8,128)S(1)}, u32[]{:S(2)}, u32[]{:S(2)}) %collective-permute-start) | collective-permute-done | bytes 348192 | tf_op jit(solution)/shard_map/ppermute | solution.py:144
  31.7 0.9 collective-permute-done.1
  32.6 7.5 %collective-permute-done.2 = f32[680,128]{1,0:T(8,128)S(1)} collective-permute-done((f32[680,128]{1,0:T(8,128)S(1)}, f32[680,128]{1,0:T(8,128)S(1)}, u32[]{:S(2)}, u32[]{:S(2)}) %collective-permute-start.2) | collective-permute-done | bytes 348192 | tf_op jit(solution)/shard_map/ppermute | solution.py:144
  40.1 0.1 pad_maximum_fusion
  40.2 0.1 broadcast_in_dim.36
  40.3 0.1 broadcast_in_dim.38
  40.4 0.1 broadcast_in_dim.39
  40.5 0.1 broadcast_in_dim.40
  40.6 0.3 fusion.3
  40.9 1.3 collective-permute-start.3
  42.2 8.5 %collective-permute-done.3 = f32[680,128]{1,0:T(8,128)S(1)} collective-permute-done((f32[680,128]{1,0:T(8,128)S(1)}, f32[680,128]{1,0:T(8,128)S(1)}, u32[]{:S(2)}, u32[]{:S(2)}) %collective-permute-start.3) | collective-permute-done | bytes 348192 | tf_op jit(solution)/shard_map/ppermute | solution.py:161
  50.7 1.3 collective-permute-start.4
  52.0 7.6 %collective-permute-done.4 = f32[680,128]{1,0:T(8,128)S(1)} collective-permute-done((f32[680,128]{1,0:T(8,128)S(1)}, f32[680,128]{1,0:T(8,128)S(1)}, u32[]{:S(2)}, u32[]{:S(2)}) %collective-permute-start.4) | collective-permute-done | bytes 348192 | tf_op jit(solution)/shard_map/ppermute | solution.py:165
  59.6 0.1 broadcast_in_dim.41
  59.7 0.1 fusion.2
  59.8 1.3 collective-permute-start.5
  61.1 18.8 %collective-permute-done.5 = f32[680,128]{1,0:T(8,128)S(1)} collective-permute-done((f32[680,128]{1,0:T(8,128)S(1)}, f32[680,128]{1,0:T(8,128)S(1)}, u32[]{:S(2)}, u32[]{:S(2)}) %collective-permute-start.5) | collective-permute-done | bytes 348192 | tf_op jit(solution)/shard_map/ppermute | solution.py:165
  79.9 0.1 broadcast_in_dim.42
  80.0 0.2 fusion.12
  80.1 0.1 broadcast_in_dim.43
  80.2 0.1 broadcast_in_dim.44
  80.3 0.2 fusion.10
  80.5 0.1 pad_maximum_fusion.1
  80.6 0.0 copy-start.1
  80.6 0.1 constant_dynamic-slice_fusion
  80.7 1.5 %collective-permute-start.6 = (f32[640,128]{1,0:T(8,128)S(1)}, f32[640,128]{1,0:T(8,128)S(1)}, u32[]{:S(2)}, u32[]{:S(2)}) collective-permute-start(f32[640,128]{1,0:T(8,128)S(1)} %get-tuple-element.33), channel_id=1, source_target_pairs={{0,2},{2,0},{4,6},{6,4},{8,10},{10,8},{12,14},{14,12},{16,18},{18,... | collective-permute-start | bytes 983048 | tf_op jit(solution)/shard_map/ppermute | solution.py:173
  82.2 0.0 collective-permute-start.7
  82.3 1.3 collective-permute-start.8
  83.5 0.0 copy-done.1
  83.5 0.1 mul.56
  83.6 5.8 %collective-permute-done.6 = f32[640,128]{1,0:T(8,128)S(1)} collective-permute-done((f32[640,128]{1,0:T(8,128)S(1)}, f32[640,128]{1,0:T(8,128)S(1)}, u32[]{:S(2)}, u32[]{:S(2)}) %collective-permute-start.6) | collective-permute-done | bytes 327712 | tf_op jit(solution)/shard_map/ppermute | solution.py:173
  89.3 8.3 %collective-permute-done.7 = f32[640,128]{1,0:T(8,128)S(1)} collective-permute-done((f32[640,128]{1,0:T(8,128)S(1)}, f32[640,128]{1,0:T(8,128)S(1)}, u32[]{:S(2)}, u32[]{:S(2)}) %collective-permute-start.7) | collective-permute-done | bytes 327712 | tf_op jit(solution)/shard_map/ppermute | solution.py:173
  97.7 0.0 collective-permute-done.8
  97.7 0.1 pad_maximum_fusion.2
  97.8 0.1 dynamic-slice_bitcast_fusion.7
  97.9 1.2 pad_maximum_fusion.3.init_ref
  99.1 27.1 %outputs.1 = (f32[2560,2048]{1,0:T(8,128)}, f32[1,2048]{1,0:T(1,128)}) custom-call(bf16[2560,2048]{1,0:T(8,128)(2,1)} %bitcast.146, bf16[2560,2048]{1,0:T(8,128)(2,1)} %bitcast.147, f32[40,2048]{1,0:T(8,128)} %bitcast.160, f32[40,1]{1,0:T(8,128)} %copy.11.bias_ref, f32[40,1]{1,0:T(8,128)} %copy.12.rate_ref, bf16[2048,128]{1,0:T(8,128)(2,1)} %b_ref.3, ...), custom_call_target="tpu_custom_call" | custom-call | tf_op jit(solution)/shard_map/outputs/pallas_call | solution.py:212
  126.1 4.0 %psum.7 = f32[1,2048]{1,0:T(1,128)S(1)} all-reduce(f32[1,2048]{1,0:T(1,128)} %get-tuple-element.14), channel_id=1, replica_groups=mesh['ctx'=16,'grp'=2] {'grp'}, use_global_device_ids=true, to_apply=%region_0.1 | all-reduce | flops 2048 | bytes 16384 | tf_op jit(solution)/shard_map/psum | solution.py:224
  130.2 12.8 %multiply_convert_fusion = bf16[2560,2048]{1,0:T(8,128)(2,1)} fusion(f32[2560,2048]{1,0:T(8,128)} %get-tuple-element.13, f32[2560]{0:T(1024)S(1)} %mul.56, f32[2048]{0:T(1024)S(1)} %bitcast.168), kind=kLoop, calls=%fused_computation | loop fusion | flops 15728640 | bytes 31475712 | tf_op jit(solution)/shard_map/convert_element_type | solution.py:227
  (5 shorter events, 0.1 us)
Async XLA Ops:
  21.1 1.4 copy-start
  22.6 9.1 %collective-permute-start = (f32[680,128]{1,0:T(8,128)S(1)}, f32[680,128]{1,0:T(8,128)S(1)}, u32[]{:S(2)}, u32[]{:S(2)}) collective-permute-start(f32[680,128]{1,0:T(8,128)S(1)} %get-tuple-element.43), channel_id=1, source_target_pairs={{0,2},{2,0},{4,6},{6,4},{8,10},{10,8},{12,14},{14,12},{16,18},{18,... | collective-permute-start | bytes 1044488 | tf_op jit(solution)/shard_map/ppermute | solution.py:144
  23.9 8.8 %collective-permute-start.1 = (f32[680,128]{1,0:T(8,128)S(1)}, f32[680,128]{1,0:T(8,128)S(1)}, u32[]{:S(2)}, u32[]{:S(2)}) collective-permute-start(f32[680,128]{1,0:T(8,128)S(1)} %get-tuple-element.44), channel_id=1, source_target_pairs={{0,4},{2,6},{4,0},{6,2},{8,12},{10,14},{12,8},{14,10},{16,20},{18,... | collective-permute-start | bytes 1044488 | tf_op jit(solution)/shard_map/ppermute | solution.py:144
  25.1 15.0 %collective-permute-start.2 = (f32[680,128]{1,0:T(8,128)S(1)}, f32[680,128]{1,0:T(8,128)S(1)}, u32[]{:S(2)}, u32[]{:S(2)}) collective-permute-start(f32[680,128]{1,0:T(8,128)S(1)} %get-tuple-element.45), channel_id=1, source_target_pairs={{0,6},{2,4},{4,2},{6,0},{8,14},{10,12},{12,10},{14,8},{16,22},{18,... | collective-permute-start | bytes 1044488 | tf_op jit(solution)/shard_map/ppermute | solution.py:144
  40.9 9.8 %collective-permute-start.3 = (f32[680,128]{1,0:T(8,128)S(1)}, f32[680,128]{1,0:T(8,128)S(1)}, u32[]{:S(2)}, u32[]{:S(2)}) collective-permute-start(f32[680,128]{1,0:T(8,128)S(1)} %pad_maximum_fusion.8), channel_id=1, source_target_pairs={{0,8},{2,10},{4,12},{6,14},{8,16},{10,18},{12,20},{14,22},{16,24},... | collective-permute-start | bytes 1044488 | tf_op jit(solution)/shard_map/ppermute | solution.py:161
  50.7 8.9 %collective-permute-start.4 = (f32[680,128]{1,0:T(8,128)S(1)}, f32[680,128]{1,0:T(8,128)S(1)}, u32[]{:S(2)}, u32[]{:S(2)}) collective-permute-start(f32[680,128]{1,0:T(8,128)S(1)} %collective-permute-done.3), channel_id=1, source_target_pairs={{0,8},{2,10},{4,12},{6,14},{8,16},{10,18},{12,20},{14,22},{16,24},... | collective-permute-start | bytes 1044488 | tf_op jit(solution)/shard_map/ppermute | solution.py:165
  59.8 20.1 %collective-permute-start.5 = (f32[680,128]{1,0:T(8,128)S(1)}, f32[680,128]{1,0:T(8,128)S(1)}, u32[]{:S(2)}, u32[]{:S(2)}) collective-permute-start(f32[680,128]{1,0:T(8,128)S(1)} %pad_maximum_fusion.9), channel_id=1, source_target_pairs={{0,16},{2,18},{4,20},{6,22},{8,24},{10,26},{12,28},{14,30},{1,17},... | collective-permute-start | bytes 1044488 | tf_op jit(solution)/shard_map/ppermute | solution.py:165
  80.6 2.9 %copy-start.1 = (f32[40,64]{1,0:T(8,128)S(1)}, f32[40,64]{1,0:T(8,128)}, u32[]{:S(2)}) copy-start(f32[40,64]{1,0:T(8,128)} %param.15) | copy-start | bytes 30724
  80.7 8.6 %collective-permute-start.6 = (f32[640,128]{1,0:T(8,128)S(1)}, f32[640,128]{1,0:T(8,128)S(1)}, u32[]{:S(2)}, u32[]{:S(2)}) collective-permute-start(f32[640,128]{1,0:T(8,128)S(1)} %get-tuple-element.33), channel_id=1, source_target_pairs={{0,2},{2,0},{4,6},{6,4},{8,10},{10,8},{12,14},{14,12},{16,18},{18,... | collective-permute-start | bytes 983048 | tf_op jit(solution)/shard_map/ppermute | solution.py:173
  82.2 15.4 %collective-permute-start.7 = (f32[640,128]{1,0:T(8,128)S(1)}, f32[640,128]{1,0:T(8,128)S(1)}, u32[]{:S(2)}, u32[]{:S(2)}) collective-permute-start(f32[640,128]{1,0:T(8,128)S(1)} %get-tuple-element.32), channel_id=1, source_target_pairs={{0,4},{2,6},{4,0},{6,2},{8,12},{10,14},{12,8},{14,10},{16,20},{18,... | collective-permute-start | bytes 983048 | tf_op jit(solution)/shard_map/ppermute | solution.py:173
  82.3 15.4 %collective-permute-start.8 = (f32[640,128]{1,0:T(8,128)S(1)}, f32[640,128]{1,0:T(8,128)S(1)}, u32[]{:S(2)}, u32[]{:S(2)}) collective-permute-start(f32[640,128]{1,0:T(8,128)S(1)} %get-tuple-element.31), channel_id=1, source_target_pairs={{0,6},{2,4},{4,2},{6,0},{8,14},{10,12},{12,10},{14,8},{16,22},{18,... | collective-permute-start | bytes 983048 | tf_op jit(solution)/shard_map/ppermute | solution.py:173

commit v2 on v1

--- a/solution.py
+++ b/solution.py
@@ -1,4 +1,5 @@
 import functools
+import math
 
 import jax
 import jax.numpy as jnp
@@ -36,13 +37,11 @@
 
 
 def scaled_rows(x_ref, w_ref, yhi_ref, ylo_ref, first, group, width):
-    for i in range(group):
-        h = first + i
-        w = w_ref[pl.ds(h, 1), :]
-        y = x_ref[pl.ds(pl.multiple_of(h * width, width), width), :].astype(F32) * w
-        hi, lo = split(y)
-        yhi_ref[i * width:(i + 1) * width, :] = hi
-        ylo_ref[i * width:(i + 1) * width, :] = lo
+    for h in range(first, first + group):
+        at = slice(h * width, (h + 1) * width)
+        hi, lo = split(x_ref[at, :].astype(F32) * w_ref[h:h + 1, :])
+        yhi_ref[at, :] = hi
+        ylo_ref[at, :] = lo
 
 
 def state_kernel(heads, width, group, x_ref, raw_ref, bias_ref, rate_ref, b_ref,
@@ -61,20 +60,17 @@
     t_ref[...] += end
     rows = group * width
 
-    def body(g, carry):
-        first = g * group
-        at = pl.ds(pl.multiple_of(first * width, width), rows)
+    b = b_ref[...]
+    for first in range(0, heads, group):
+        at = slice(first * width, first * width + rows)
         scaled_rows(x_ref, w_ref, yhi_ref, ylo_ref, first, group, width)
-        part = dot(yhi_ref[...], b_ref[...]) + dot(ylo_ref[...], b_ref[...])
+        part = dot(yhi_ref[at, :], b) + dot(ylo_ref[at, :], b)
         old = s_ref[at, :]
         loc_ref[0, at, :] = old
         new = old + part
         for i in range(group):
-            s_ref[pl.ds(pl.multiple_of((first + i) * width, width), width), :] = (
-                new[i * width:(i + 1) * width, :] * e_ref[pl.ds(first + i, 1), :])
-        return carry
-
-    lax.fori_loop(0, heads // group, body, 0)
+            h = first + i
+            s_ref[h * width:(h + 1) * width, :] = new[i * width:(i + 1) * width, :] * e_ref[h:h + 1, :]
     last_ref[...] = s_ref[...]
     log_ref[...] = t_ref[...]
 
@@ -100,79 +96,169 @@
     mhi, mlo = split(jnp.where(causal, scores, 0.0))
     twice = jnp.concatenate([c_ref[...], c_ref[...]], axis=1)
 
-    def body(g, total):
-        first = g * group
+    total = jnp.zeros((8, q), F32)
+    for first in range(0, heads, group):
+        block = slice(first * width, first * width + rows)
         scaled_rows(x_ref, w_ref, yhi_ref, ylo_ref, first, group, width)
+        for h in range(first, first + group):
+            at = slice(h * width, (h + 1) * width)
+            hi, lo = split(loc_ref[0, at, :] + init_ref[at, :] * d_ref[h:h + 1, :])
+            shl_ref[at, :n] = hi
+            shl_ref[at, n:] = lo
+        mixed = (dot(yhi_ref[block, :], mhi) + dot(ylo_ref[block, :], mhi) + dot(yhi_ref[block, :], mlo)
+                 + lax.dot_general(shl_ref[block, :], twice, NT, preferred_element_type=F32))
         for i in range(group):
-            at = pl.ds(pl.multiple_of((first + i) * width, width), width)
-            s = loc_ref[0, at, :] + init_ref[at, :] * d_ref[pl.ds(first + i, 1), :]
-            hi, lo = split(s)
-            shl_ref[i * width:(i + 1) * width, :n] = hi
-            shl_ref[i * width:(i + 1) * width, n:] = lo
-        mixed = (dot(yhi_ref[...], mhi) + dot(ylo_ref[...], mhi) + dot(yhi_ref[...], mlo)
-                 + lax.dot_general(shl_ref[...], twice, NT, preferred_element_type=F32))
-        for i in range(group):
-            at = pl.ds(pl.multiple_of((first + i) * width, width), width)
+            h = first + i
+            at = slice(h * width, (h + 1) * width)
             v = gate_ref[at, :].astype(F32)
             half = 0.5 * v
             silu = half + half * jnp.tanh(half)
-            gated = mixed[i * width:(i + 1) * width, :] * e_ref[pl.ds(first + i, 1), :] * silu
+            gated = mixed[i * width:(i + 1) * width, :] * e_ref[h:h + 1, :] * silu
             out_ref[at, :] = gated
             total = total + jnp.sum((gated * gated).reshape(width // 8, 8, q), axis=0)
-        return total
-
-    total = lax.fori_loop(0, heads // group, body, jnp.zeros((8, q), F32))
     sq_ref[...] = jnp.sum(total, axis=0, keepdims=True)
 
 
-def group_of(heads, most=10):
+def group_of(heads, most=5):
     return max(k for k in range(1, most + 1) if heads % k == 0)
 
 
+def carry_kernel(count, inner, pieces, width, last_ref, log_ref, out_ref,
+                 got_ref, dgot_ref, ent_ref, nxt_ref, fin_ref, ret_ref,
+                 d_send, d_recv, a_send, a_recv, z_send, z_recv, c_send, c_recv):
+    here = lax.axis_index("ctx")
+    me, plane, planes = lax.rem(here, inner), here // inner, count // inner
+    base = here - me
+    part = got_ref.shape[1]
+    size = part // pieces
+    step = math.gcd(size, width)
+    mesh = pl.DeviceIdType.MESH
+    to = [base + lax.rem(me + k, inner) for k in range(inner)]
+    first, final = plane == 0, plane == planes - 1
+
+    barrier = pltpu.get_barrier_semaphore()
+    for k in range(1, inner):
+        pl.semaphore_signal(barrier, inc=1, device_id={"ctx": to[k]}, device_id_type=mesh)
+
+    @pl.when(jnp.logical_not(first))
+    def _():
+        pl.semaphore_signal(barrier, inc=1, device_id={"ctx": here - inner}, device_id_type=mesh)
+
+    @pl.when(jnp.logical_not(final))
+    def _():
+        pl.semaphore_signal(barrier, inc=1, device_id={"ctx": here + inner}, device_id_type=mesh)
+
+    inside = jnp.logical_and(jnp.logical_not(first), jnp.logical_not(final))
+    alone = jnp.logical_and(first, final)
+
+    @pl.when(inside)
+    def _():
+        pl.semaphore_wait(barrier, inner + 1)
+
+    @pl.when(alone)
+    def _():
+        pl.semaphore_wait(barrier, inner - 1)
+
+    @pl.when(jnp.logical_not(jnp.logical_or(inside, alone)))
+    def _():
+        pl.semaphore_wait(barrier, inner)
+
+    def remote(src, dst, send, recv, device):
+        return pltpu.make_async_remote_copy(src_ref=src, dst_ref=dst, send_sem=send, recv_sem=recv,
+                                            device_id={"ctx": device}, device_id_type=mesh)
+
+    def rows_of(s):
+        return pl.ds(s * size, size)
+
+    logs = [remote(log_ref, dgot_ref.at[k], d_send.at[k], d_recv.at[k], to[k]) for k in range(1, inner)]
+    for copy in logs:
+        copy.start()
+    owned = [lax.rem(me + k, inner) * part for k in range(inner)]
+    out_copies = {}
+    for s in range(pieces):
+        for k in range(1, inner):
+            out_copies[s, k] = remote(
+                last_ref.at[pl.ds(pl.multiple_of(owned[k] + s * size, step), size), :],
+                got_ref.at[k, rows_of(s), :], a_send.at[k, s], a_recv.at[k, s], to[k])
+            out_copies[s, k].start()
+    got_ref[0] = last_ref[pl.ds(pl.multiple_of(owned[0], step), part), :]
+    dgot_ref[0] = log_ref[...]
+
+    @pl.when(first)
+    def _():
+        ent_ref[...] = jnp.zeros_like(ent_ref)
+
+    for copy in logs:
+        copy.wait()
+    chain, back = [], []
+    for s in range(pieces):
+        for k in range(1, inner):
+            out_copies[s, k].wait()
+        link = remote(nxt_ref.at[rows_of(s), :], ent_ref.at[rows_of(s), :],
+                      z_send.at[s], z_recv.at[s], here + inner)
+
+        @pl.when(jnp.logical_not(first))
+        def _():
+            link.wait_recv()
+
+        for r in range(s * size, (s + 1) * size, step):
+            at = slice(r, r + step)
+            head = (owned[0] + r) // width
+            state = ent_ref[at, :]
+            for j in range(inner):
+                fin_ref[j, at, :] = state
+                slot = lax.rem(me - j + inner, inner)
+                state = state * jnp.exp(dgot_ref[slot, pl.ds(head, 1), :]) + got_ref[slot, at, :]
+            nxt_ref[at, :] = state
+
+        @pl.when(jnp.logical_not(final))
+        def _():
+            link.start()
+
+        for k in range(1, inner):
+            copy = remote(fin_ref.at[lax.rem(me + k, inner), rows_of(s), :], ret_ref.at[k, rows_of(s), :],
+                          c_send.at[k, s], c_recv.at[k, s], to[k])
+            copy.start()
+            back.append(copy)
+        chain.append(link)
+
+    out_ref[pl.ds(pl.multiple_of(owned[0], step), part), :] = fin_ref[me]
+
+    @pl.when(jnp.logical_not(final))
+    def _():
+        for link in chain:
+            link.wait_send()
+
+    for copy in back:
+        copy.wait()
+    for k in range(1, inner):
+        owner = lax.rem(me - k + inner, inner)
+        out_ref[pl.ds(pl.multiple_of(owner * part, step), part), :] = ret_ref[k]
+
+
 def carry(last, logs, width):
-    count, here = lax.axis_size("ctx"), lax.axis_index("ctx")
-    inner = 4 if count % 4 == 0 else 2 if count % 2 == 0 else 1
-    outer = count // inner
+    count = lax.axis_size("ctx")
+    inner = 4 if count % 4 == 0 else 2
     rows, n = last.shape
-    heads = logs.shape[0]
     part = rows // inner
-    me = here % inner
-    parts = last.reshape(inner, part, n)
-    wide = [jnp.concatenate([lax.dynamic_index_in_dim(parts, me ^ k, 0, False), logs], 0)
-            for k in range(inner)]
-    got = [wide[0]] + [
-        lax.ppermute(wide[k], "ctx", [(i, i ^ k) for i in range(count)]) for k in range(1, inner)]
-    got = jnp.stack(got)
-
-    def spread(log):
-        long = jnp.repeat(log, width, axis=0).reshape(inner, part, n)
-        return lax.dynamic_index_in_dim(long, me, 0, False)
-
-    before, prefix, since = jnp.zeros((part, n), F32), [], jnp.zeros((heads, n), F32)
-    logs_before = []
-    for k in range(inner):
-        piece = lax.dynamic_index_in_dim(got, me ^ k, 0, False)
-        prefix.append(before)
-        logs_before.append(since)
-        log = piece[part:]
-        before = before * jnp.exp(spread(log)) + piece[:part]
-        since = since + log
-    total, total_log = before, since
-    acc = lax.ppermute(jnp.concatenate([total, total_log], 0), "ctx",
-                       [(i, i + inner) for i in range(count - inner)])
-    shift = 1
-    while shift < outer - 1:
-        earlier = lax.ppermute(acc, "ctx", [(i, i + shift * inner) for i in range(count - shift * inner)])
-        state = acc[:part] + jnp.exp(spread(acc[part:])) * earlier[:part]
-        acc = jnp.concatenate([state, acc[part:] + earlier[part:]], 0)
-        shift *= 2
-    entering = acc[:part]
-    finals = jnp.stack([p + jnp.exp(spread(l)) * entering for p, l in zip(prefix, logs_before)])
-    mine = [lax.dynamic_index_in_dim(finals, me ^ k, 0, False) for k in range(inner)]
-    back = [mine[0]] + [
-        lax.ppermute(mine[k], "ctx", [(i, i ^ k) for i in range(count)]) for k in range(1, inner)]
-    back = jnp.stack(back)
-    return jnp.concatenate([lax.dynamic_index_in_dim(back, me ^ k, 0, False) for k in range(inner)], 0)
+    pieces = 5 if part % 160 == 0 else 1
+    vmem = pl.BlockSpec(memory_space=pltpu.VMEM)
+    sems = [pltpu.SemaphoreType.DMA((inner,))] * 2
+    sems += [pltpu.SemaphoreType.DMA((inner, pieces))] * 2
+    sems += [pltpu.SemaphoreType.DMA((pieces,))] * 2
+    sems += [pltpu.SemaphoreType.DMA((inner, pieces))] * 2
+    return pl.pallas_call(
+        functools.partial(carry_kernel, count, inner, pieces, width),
+        out_shape=jax.ShapeDtypeStruct((rows, n), F32),
+        in_specs=[vmem, vmem],
+        out_specs=vmem,
+        scratch_shapes=[pltpu.VMEM((inner, part, n), F32), pltpu.VMEM((inner,) + logs.shape, F32),
+                        pltpu.VMEM((part, n), F32), pltpu.VMEM((part, n), F32),
+                        pltpu.VMEM((inner, part, n), F32), pltpu.VMEM((inner, part, n), F32)] + sems,
+        compiler_params=pltpu.CompilerParams(collective_id=0, has_side_effects=True,
+                                             vmem_limit_bytes=40 << 20),
+        name="carry",
+    )(last, logs)
 
 
 def shards(head_inputs, gate_inputs, step_raw, step_bias, decay_rate, input_proj, output_proj, norm_gain):
@@ -192,7 +278,7 @@
     proj = pl.BlockSpec((BLOCK, n), lambda c: (c, 0))
     local = pl.BlockSpec((1, rows, n), lambda c: (c, 0, 0))
     params = pltpu.CompilerParams(dimension_semantics=("arbitrary",), vmem_limit_bytes=60 << 20)
-    ys = [pltpu.VMEM((group * width, BLOCK), BF16)] * 2
+    ys = [pltpu.VMEM((rows, BLOCK), BF16)] * 2
 
     loc, last, logs = pl.pallas_call(
         functools.partial(state_kernel, heads, width, group),
@@ -217,7 +303,7 @@
         out_shape=[jax.ShapeDtypeStruct((rows, tokens), F32), jax.ShapeDtypeStruct((1, tokens), F32)],
         scratch_shapes=[pltpu.VMEM((heads, BLOCK), F32), pltpu.VMEM((heads, BLOCK), F32),
                         pltpu.VMEM((heads, n), F32), pltpu.VMEM((heads, n), F32)] + ys
-                       + [pltpu.VMEM((group * width, 2 * n), BF16)],
+                       + [pltpu.VMEM((rows, 2 * n), BF16)],
         compiler_params=params, name="outputs",
     )(x, gate, raw, bias, rate, input_proj, output_proj, loc, init)
 

time: 143 us -> 97.1 us (0.68); the launches traced: 143 us -> 95.3 us
  waiting for transfers between devices: 63.8 us -> 0 us
  Pallas kernels: 45.5 us -> 72.3 us
  starting transfers between devices: 9.38 us -> 0 us
  other arithmetic: 15.2 us -> 12.8 us
    ppermute x9 -> x0, waiting for transfers between devices: 63.8 us -> none  [the longest x2 26.4 us: carry(): lax.ppermute(acc, 'ctx', [(i, i + shift * inner) for i in range(count - s...]
    pallas_call x0 -> x1, Pallas kernels: none -> 32.2 us  [carry(): pl.pallas_call(functools.partial(carry_kernel, count, inner, pieces, widt...]
    ppermute x9 -> x0, starting transfers between devices: 9.38 us -> none  [the longest x3 2.81 us: carry(): lax.ppermute(mine[k], 'ctx', [(i, i ^ k) for i in range(count)])]
    pallas_call x1, Pallas kernels: 18.4 us -> 14.7 us  [shards(): pl.pallas_call(functools.partial(state_kernel, heads, width, group), grid...]
    unnamed x4 -> x8, local copies, waits for them, and re-layouts: 0.01 us -> 3.09 us
    pallas_call x1, Pallas kernels: 27.1 us -> 25.3 us  [shards(): pl.pallas_call(functools.partial(output_kernel, heads, width, group), gri...]
    squeeze x2 -> x0, local copies, waits for them, and re-layouts: 1.47 us -> none  [the longest x1 1.38 us: carry(): lax.dynamic_index_in_dim(parts, me ^ k, 0, False)]
  transfers between devices with their start and end apart: 9 -> 0, of which waited for: 8 -> 0; matrix products, arithmetic and copies ran while one was open for 0% -> 0% of each run, Pallas kernels for 0% -> 0%
where the time goes in v2:
time: 97.1 us; the launch traced here: 95.3 us
  Pallas kernels  72.3 us (74%)
  other arithmetic  12.8 us (13%)
  local copies, waits for them, and re-layouts  5.83 us (6%)
  blocking collectives  4.31 us (4%)
    pallas_call x1, Pallas kernels, carry(): pl.pallas_call(functools.partial(carry_kernel, count, inner, pieces, widt...  32.2 us
    pallas_call x1, Pallas kernels, shards(): pl.pallas_call(functools.partial(output_kernel, heads, width, group), gri...  25.3 us
    pallas_call x1, Pallas kernels, shards(): pl.pallas_call(functools.partial(state_kernel, heads, width, group), grid...  14.7 us
    convert_element_type x1, other arithmetic, shards(): result = (gated * scale * norm_gain.reshape(rows, 1)).astype(BF16)  12.8 us
    psum x1, blocking collectives, shards(): total_sq = lax.psum(local_sq, 'grp')  4.31 us
    unnamed x8, local copies, waits for them, and re-layouts  3.09 us
    broadcast_in_dim x2, local copies, waits for them, and re-layouts, shards(): bias, rate = (step_bias[:, None], decay_rate[:, None])  2.67 us

profile of v2, /device:TPU:25, one launch (start us, length us, event | category | flops | bytes accessed | tf_op | source)
XLA Modules:
  0.0 95.3 jit_solution(10152209672708455394)
XLA Ops:
  0.0 1.3 %copy.11.bias_ref = f32[40,1]{1,0:T(8,128)} copy(f32[40,1]{0,1:T(1,128)} %bitcast.19) | data formatting | bytes 320 | tf_op jit(solution)/shard_map/broadcast_in_dim | solution.py:273
  1.3 1.3 %copy.12.rate_ref = f32[40,1]{1,0:T(8,128)} copy(f32[40,1]{0,1:T(1,128)} %bitcast.20) | data formatting | bytes 320 | tf_op jit(solution)/shard_map/broadcast_in_dim | solution.py:273
  2.7 14.7 %local_state.1 = (f32[8,2560,128]{2,1,0:T(8,128)}, f32[2560,128]{1,0:T(8,128)}, f32[40,128]{1,0:T(8,128)}) custom-call(bf16[2560,2048]{1,0:T(8,128)(2,1)} %bitcast.13, f32[40,2048]{1,0:T(8,128)} %bitcast.16, f32[40,1]{1,0:T(8,128)} %copy.11.bias_ref, f32[40,1]{1,0:T(8,128)} %copy.12.rate_ref, bf16[2048,128]{1,0:T(8,128)(2,1)} %b_ref.3), custom_call_target="tpu_custom_call" | custom-call | tf_op jit(solution)/shard_map/local_state/pallas_call | solution.py:283
  17.4 0.0 copy-start.1
  17.4 1.3 %copy-done.1 = f32[2560,128]{1,0:T(8,128)S(1)} copy-done((f32[2560,128]{1,0:T(8,128)S(1)}, f32[2560,128]{1,0:T(8,128)}, u32[]{:S(2)}) %copy-start.1) | copy-done | bytes 1310744
  18.7 0.0 copy-start.2
  18.7 0.7 copy-done.2
  19.4 32.2 %carry.1.init_ref = f32[2560,128]{1,0:T(8,128)S(1)} custom-call(f32[2560,128]{1,0:T(8,128)S(1)} %copy-done.1, f32[40,128]{1,0:T(8,128)S(1)} %copy-done.2), custom_call_target="tpu_custom_call" | custom-call | tf_op jit(solution)/shard_map/carry/pallas_call | solution.py:250
  51.6 0.0 copy-start
  51.6 1.0 %copy-done = f32[2560,128]{1,0:T(8,128)} copy-done((f32[2560,128]{1,0:T(8,128)}, f32[2560,128]{1,0:T(8,128)S(1)}, u32[]{:S(2)}) %copy-start) | copy-done | bytes 1310744
  52.7 0.0 copy-start.3
  52.7 25.3 %outputs.1 = (f32[2560,2048]{1,0:T(8,128)}, f32[1,2048]{1,0:T(1,128)}) custom-call(bf16[2560,2048]{1,0:T(8,128)(2,1)} %bitcast.14, bf16[2560,2048]{1,0:T(8,128)(2,1)} %bitcast.15, f32[40,2048]{1,0:T(8,128)} %bitcast.17, f32[40,1]{1,0:T(8,128)} %copy.11.bias_ref, f32[40,1]{1,0:T(8,128)} %copy.12.rate_ref, bf16[2048,128]{1,0:T(8,128)(2,1)} %b_ref.3, ...), custom_call_target="tpu_custom_call" | custom-call | tf_op jit(solution)/shard_map/outputs/pallas_call | solution.py:298
  78.0 4.3 %psum.7 = f32[1,2048]{1,0:T(1,128)S(1)} all-reduce(f32[1,2048]{1,0:T(1,128)} %get-tuple-element.14), channel_id=1, replica_groups=mesh['ctx'=16,'grp'=2] {'grp'}, use_global_device_ids=true, to_apply=%region_0.0 | all-reduce | flops 2048 | bytes 16384 | tf_op jit(solution)/shard_map/psum | solution.py:310
  82.4 0.0 copy-done.3
  82.4 0.1 mul.23
  82.5 12.8 %multiply_convert_fusion = bf16[2560,2048]{1,0:T(8,128)(2,1)} fusion(f32[2560,2048]{1,0:T(8,128)} %get-tuple-element.13, f32[2560]{0:T(1024)S(1)} %mul.23, f32[2048]{0:T(1024)S(1)} %bitcast.18), kind=kLoop, calls=%fused_computation | loop fusion | flops 15728640 | bytes 31475712 | tf_op jit(solution)/shard_map/convert_element_type | solution.py:313
  (1 shorter events, 0.0 us)
Async XLA Ops:
  17.4 1.3 %copy-start.1 = (f32[2560,128]{1,0:T(8,128)S(1)}, f32[2560,128]{1,0:T(8,128)}, u32[]{:S(2)}) copy-start(f32[2560,128]{1,0:T(8,128)} %get-tuple-element.11.last_ref) | copy-start | bytes 3932164
  18.7 0.7 copy-start.2
  51.6 1.1 %copy-start = (f32[2560,128]{1,0:T(8,128)}, f32[2560,128]{1,0:T(8,128)S(1)}, u32[]{:S(2)}) copy-start(f32[2560,128]{1,0:T(8,128)S(1)} %carry.1.init_ref) | copy-start | bytes 3932164
  52.7 29.7 %copy-start.3 = (f32[40,64]{1,0:T(8,128)S(1)}, f32[40,64]{1,0:T(8,128)}, u32[]{:S(2)}) copy-start(f32[40,64]{1,0:T(8,128)} %param.15) | copy-start | bytes 30724

commit v3 on v2

v3 whole, which is shorter than its diff:
```python
import functools
import math

import jax
import jax.numpy as jnp
from jax import lax
from jax.experimental import pallas as pl
from jax.experimental.pallas import tpu as pltpu
from jax.sharding import PartitionSpec as P

BLOCK = 256
EPS = 1e-05
NT = (((1,), (1,)), ((), ()))
F32, BF16 = jnp.float32, jnp.bfloat16


def dot(a, b):
    return jnp.dot(a, b, preferred_element_type=F32)


def split(v):
    hi = v.astype(BF16)
    return hi, (v - hi.astype(F32)).astype(BF16)


def decays(raw, bias, rate):
    v = raw + bias
    step = jnp.maximum(v, 0.0) + jnp.log1p(jnp.exp(-jnp.abs(v)))
    log = -rate * step
    q = raw.shape[1]
    upto = lax.broadcasted_iota(jnp.int32, (q, q), 0) <= lax.broadcasted_iota(jnp.int32, (q, q), 1)
    upto = upto.astype(BF16)
    a, rest = log.astype(BF16), log - log.astype(BF16).astype(F32)
    b, c = split(rest)
    running = dot(a, upto) + dot(b, upto) + dot(c, upto)
    return step, running


def scaled_rows(x_ref, w_ref, now, yhi_ref, ylo_ref, first, group, width):
    for h in range(first, first + group):
        at = slice(h * width, (h + 1) * width)
        hi, lo = split(x_ref[at, :].astype(F32) * w_ref[h:h + 1, now])
        yhi_ref[at, :] = hi
        ylo_ref[at, :] = lo


def state_kernel(heads, width, group, x_ref, raw_ref, head_ref, b_ref,
                 loc_ref, last_ref, log_ref, w_ref, e_ref, reach_ref,
                 s_ref, end_ref, yhi_ref, ylo_ref):
    c = pl.program_id(0)
    q, n = b_ref.shape

    @pl.when(c == 0)
    def _():
        s_ref[...] = jnp.zeros_like(s_ref)
        since = jnp.zeros((heads, 1), F32)
        for k in range(pl.num_programs(0)):
            at = slice(k * q, (k + 1) * q)
            step, running = decays(raw_ref[:, at], head_ref[:, :1], head_ref[:, 1:])
            w_ref[:, at] = step * jnp.exp(-running)
            e_ref[:, at] = jnp.exp(running)
            reach_ref[:, at] = jnp.exp(running + since)
            end_ref[k] = jnp.exp(jnp.broadcast_to(running[:, -1:], (heads, n)))
            since = since + running[:, -1:]
        log_ref[...] = jnp.broadcast_to(since, log_ref.shape)

    b = b_ref[...]
    rows = group * width
    now = pl.ds(pl.multiple_of(c * q, q), q)
    for first in range(0, heads, group):
        at = slice(first * width, first * width + rows)
        scaled_rows(x_ref, w_ref, now, yhi_ref, ylo_ref, first, group, width)
        part = dot(yhi_ref[at, :], b) + dot(ylo_ref[at, :], b)
        old = s_ref[at, :]
        loc_ref[0, at, :] = old
        new = old + part
        for i in range(group):
            h = first + i
            s_ref[h * width:(h + 1) * width, :] = new[i * width:(i + 1) * width, :] * end_ref[c, h:h + 1, :]
    last_ref[...] = s_ref[...]


def group_of(heads, most=5):
    return max(k for k in range(1, most + 1) if heads % k == 0)


def output_kernel(count, others, inner, pieces, heads, width, group, blocks,
                  x_ref, gate_ref, w_ref, e_ref, reach_ref, b_ref, c_ref, loc_ref, last_ref, log_ref, gain_ref,
                  res_ref,
                  part_ref, yhi_ref, ylo_ref, shl_ref, init_ref, sq_ref, sqgot_ref,
                  got_ref, dgot_ref, ent_ref, nxt_ref, fin_ref, ret_ref,
                  d_send, d_recv, a_send, a_recv, z_send, z_recv, c_send, c_recv, g_send, g_recv):
    t = pl.program_id(0)
    core = lax.axis_index("grp")
    q, n = b_ref.shape
    rows = group * width
    here = lax.axis_index("ctx")
    me, plane, planes = lax.rem(here, inner), here // inner, count // inner
    base = here - me
    part = got_ref.shape[1]
    size = part // pieces
    step = math.gcd(size, width)
    mesh = pl.DeviceIdType.MESH
    to = [base + lax.rem(me + k, inner) for k in range(inner)]
    first, final = plane == 0, plane == planes - 1

    def remote(src, dst, send, recv, device):
        return pltpu.make_async_remote_copy(src_ref=src, dst_ref=dst, send_sem=send, recv_sem=recv,
                                            device_id={"ctx": device}, device_id_type=mesh)

    def rows_of(s):
        return pl.ds(s * size, size)

    owned = [lax.rem(me + k, inner) * part for k in range(inner)]
    logs = [remote(log_ref, dgot_ref.at[k], d_send.at[k], d_recv.at[k], to[k]) for k in range(1, inner)]

    def outgoing(s, k):
        return remote(last_ref.at[pl.ds(pl.multiple_of(owned[k] + s * size, step), size), :],
                      got_ref.at[k, rows_of(s), :], a_send.at[k, s], a_recv.at[k, s], to[k])

    def link_of(s):
        return remote(nxt_ref.at[rows_of(s), :], ent_ref.at[rows_of(s), :],
                      z_send.at[s], z_recv.at[s], here + inner)

    def returning(s, k):
        return remote(fin_ref.at[lax.rem(me + k, inner), rows_of(s), :], ret_ref.at[k, rows_of(s), :],
                      c_send.at[k, s], c_recv.at[k, s], to[k])

    def partner(k, c):
        return pltpu.make_async_remote_copy(
            src_ref=sq_ref.at[c], dst_ref=sqgot_ref.at[k, c], send_sem=g_send.at[k, c], recv_sem=g_recv.at[k, c],
            device_id={"grp": lax.rem(core + k, others)}, device_id_type=mesh)

    @pl.when(t == 0)
    def _():
        barrier = pltpu.get_barrier_semaphore()
        for k in range(1, inner):
            pl.semaphore_signal(barrier, inc=1, device_id={"ctx": to[k]}, device_id_type=mesh)

        for k in range(1, others):
            pl.semaphore_signal(barrier, inc=1, device_id={"grp": lax.rem(core + k, others)}, device_id_type=mesh)

        @pl.when(jnp.logical_not(first))
        def _():
            pl.semaphore_signal(barrier, inc=1, device_id={"ctx": here - inner}, device_id_type=mesh)

        @pl.when(jnp.logical_not(final))
        def _():
            pl.semaphore_signal(barrier, inc=1, device_id={"ctx": here + inner}, device_id_type=mesh)

        inside = jnp.logical_and(jnp.logical_not(first), jnp.logical_not(final))
        alone = jnp.logical_and(first, final)

        @pl.when(inside)
        def _():
            pl.semaphore_wait(barrier, inner + others)

        @pl.when(alone)
        def _():
            pl.semaphore_wait(barrier, inner + others - 2)

        @pl.when(jnp.logical_not(jnp.logical_or(inside, alone)))
        def _():
            pl.semaphore_wait(barrier, inner + others - 1)

        for copy in logs:
            copy.start()
        for s in range(pieces):
            for k in range(1, inner):
                outgoing(s, k).start()
        got_ref[0] = last_ref[pl.ds(pl.multiple_of(owned[0], step), part), :]
        dgot_ref[0] = log_ref[...]

        @pl.when(first)
        def _():
            ent_ref[...] = jnp.zeros_like(ent_ref)

    @pl.when(t < blocks)
    def _():
        scores = lax.dot_general(b_ref[...], c_ref[...], NT, preferred_element_type=F32)
        causal = lax.broadcasted_iota(jnp.int32, (q, q), 0) <= lax.broadcasted_iota(jnp.int32, (q, q), 1)
        mhi, mlo = split(jnp.where(causal, scores, 0.0))
        twice = jnp.concatenate([c_ref[...], c_ref[...]], axis=1)
        for lead in range(0, heads, group):
            block = slice(lead * width, lead * width + rows)
            scaled_rows(x_ref, w_ref, slice(None), yhi_ref, ylo_ref, lead, group, width)
            hi, lo = split(loc_ref[0, block, :])
            shl_ref[block, :n] = hi
            shl_ref[block, n:] = lo
            part_ref[t, block, :] = (
                dot(yhi_ref[block, :], mhi) + dot(ylo_ref[block, :], mhi) + dot(yhi_ref[block, :], mlo)
                + lax.dot_general(shl_ref[block, :], twice, NT, preferred_element_type=F32))

    def exchange(s):
        if s == 0:
            for copy in logs:
                copy.wait()
        for k in range(1, inner):
            outgoing(s, k).wait()

        @pl.when(jnp.logical_not(first))
        def _():
            link_of(s).wait_recv()

        for r in range(s * size, (s + 1) * size, step):
            at = slice(r, r + step)
            head = (owned[0] + r) // width
            state = ent_ref[at, :]
            for j in range(inner):
                fin_ref[j, at, :] = state
                slot = lax.rem(me - j + inner, inner)
                state = state * jnp.exp(dgot_ref[slot, pl.ds(head, 1), :]) + got_ref[slot, at, :]
            nxt_ref[at, :] = state

        @pl.when(jnp.logical_not(final))
        def _():
            link_of(s).start()

        for k in range(1, inner):
            returning(s, k).start()

    for s in range(pieces):
        @pl.when(t == min(2 * s + 1 - s // 2, blocks - 1))
        def _():
            exchange(s)

    @pl.when(t == blocks)
    def _():
        @pl.when(jnp.logical_not(final))
        def _():
            for s in range(pieces):
                link_of(s).wait_send()

        for s in range(pieces):
            for k in range(1, inner):
                returning(s, k).wait()
        for k in range(inner):
            owner = lax.rem(me - k + inner, inner)
            hi, lo = split(fin_ref[me] if k == 0 else ret_ref[k])
            at = pl.ds(pl.multiple_of(owner * part, step), part)
            init_ref[at, :n] = hi
            init_ref[at, n:] = lo

    @pl.when(jnp.logical_and(t >= blocks, t < 2 * blocks))
    def _():
        now = t - blocks
        twice = jnp.concatenate([c_ref[...], c_ref[...]], axis=1)
        total = jnp.zeros((8, q), F32)
        for lead in range(0, heads, group):
            block = slice(lead * width, lead * width + rows)
            entered = lax.dot_general(init_ref[block, :], twice, NT, preferred_element_type=F32)
            for i in range(group):
                h = lead + i
                at = slice(h * width, (h + 1) * width)
                half = 0.5 * gate_ref[at, :].astype(F32)
                silu = half + half * jnp.tanh(half)
                gated = (part_ref[now, at, :] * e_ref[h:h + 1, :]
                         + entered[i * width:(i + 1) * width, :] * reach_ref[h:h + 1, :]) * silu
                part_ref[now, at, :] = gated
                total = total + jnp.sum((gated * gated).reshape(width // 8, 8, q), axis=0)
        sq_ref[now] = jnp.broadcast_to(jnp.sum(total, axis=0, keepdims=True), (8, q))
        for k in range(1, others):
            partner(k, now).start()

    @pl.when(t > blocks)
    def _():
        past = t - blocks - 1
        for k in range(1, others):
            partner(k, past).wait()
        total = sq_ref[past]
        for k in range(1, others):
            total = total + sqgot_ref[k, past]
        scale = lax.rsqrt(total[:1, :] / (others * heads * width) + EPS)
        for lead in range(0, heads, group):
            block = slice(lead * width, lead * width + rows)
            res_ref[block, :] = (part_ref[past, block, :] * scale * gain_ref[block, :]).astype(BF16)


def shards(head_inputs, gate_inputs, step_raw, step_bias, decay_rate, input_proj, output_proj, norm_gain):
    tokens, heads, width = head_inputs.shape
    n = input_proj.shape[1]
    rows = heads * width
    blocks = tokens // BLOCK
    group = group_of(heads)
    x = jnp.transpose(head_inputs, (1, 2, 0)).reshape(rows, tokens)
    gate = jnp.transpose(gate_inputs, (1, 2, 0)).reshape(rows, tokens)
    raw = step_raw.T
    per = jnp.stack([step_bias, decay_rate], axis=1)

    wide = pl.BlockSpec((rows, BLOCK), lambda c: (0, c))
    whole = lambda *shape: pl.BlockSpec(shape, lambda c: (0,) * len(shape))
    proj = pl.BlockSpec((BLOCK, n), lambda c: (c, 0))
    local = pl.BlockSpec((1, rows, n), lambda c: (c, 0, 0))
    params = pltpu.CompilerParams(dimension_semantics=("arbitrary",), vmem_limit_bytes=60 << 20)
    ys = [pltpu.VMEM((rows, BLOCK), BF16)] * 2

    loc, last, logs, w, e, reach = pl.pallas_call(
        functools.partial(state_kernel, heads, width, group),
        grid=(blocks,),
        in_specs=[wide, whole(heads, tokens), whole(heads, 2), proj],
        out_specs=[local, whole(rows, n), whole(heads, n)] + [whole(heads, tokens)] * 3,
        out_shape=[jax.ShapeDtypeStruct((blocks, rows, n), F32),
                   jax.ShapeDtypeStruct((rows, n), F32),
                   jax.ShapeDtypeStruct((heads, n), F32)]
                  + [jax.ShapeDtypeStruct((heads, tokens), F32)] * 3,
        scratch_shapes=[pltpu.VMEM((rows, n), F32), pltpu.VMEM((blocks, heads, n), F32)] + ys,
        compiler_params=params, name="local_state",
    )(x, raw, per, input_proj)

    count, others = lax.axis_size("ctx"), lax.axis_size("grp")
    inner = 4 if count % 4 == 0 else 2
    part = rows // inner
    pieces = 5 if part % 160 == 0 else 1
    early = lambda t: jnp.minimum(t, blocks - 1)
    late = lambda t: jnp.clip(t - blocks, 0, blocks - 1)
    both = lambda t: lax.rem(jnp.minimum(t, 2 * blocks - 1), blocks)
    sems = [pltpu.SemaphoreType.DMA((inner,))] * 2
    sems += [pltpu.SemaphoreType.DMA((inner, pieces))] * 2
    sems += [pltpu.SemaphoreType.DMA((pieces,))] * 2
    sems += [pltpu.SemaphoreType.DMA((inner, pieces))] * 2
    sems += [pltpu.SemaphoreType.DMA((others, blocks))] * 2
    result = pl.pallas_call(
        functools.partial(output_kernel, count, others, inner, pieces, heads, width, group, blocks),
        grid=(2 * blocks + 1,),
        in_specs=[pl.BlockSpec((rows, BLOCK), lambda t: (0, early(t))),
                  pl.BlockSpec((rows, BLOCK), lambda t: (0, late(t))),
                  pl.BlockSpec((heads, BLOCK), lambda t: (0, early(t))),
                  pl.BlockSpec((heads, BLOCK), lambda t: (0, late(t))),
                  pl.BlockSpec((heads, BLOCK), lambda t: (0, late(t))),
                  pl.BlockSpec((BLOCK, n), lambda t: (early(t), 0)),
                  pl.BlockSpec((BLOCK, n), lambda t: (both(t), 0)),
                  pl.BlockSpec((1, rows, n), lambda t: (early(t), 0, 0)),
                  pl.BlockSpec(memory_space=pltpu.VMEM), pl.BlockSpec(memory_space=pltpu.VMEM),
                  whole(rows, 1)],
        out_specs=pl.BlockSpec((rows, BLOCK), lambda t: (0, jnp.clip(t - blocks - 1, 0, blocks - 1))),
        out_shape=jax.ShapeDtypeStruct((rows, tokens), BF16),
        scratch_shapes=[pltpu.VMEM((blocks, rows, BLOCK), F32)] + ys
                       + [pltpu.VMEM((rows, 2 * n), BF16), pltpu.VMEM((rows, 2 * n), BF16),
                          pltpu.VMEM((blocks, 8, BLOCK), F32), pltpu.VMEM((others, blocks, 8, BLOCK), F32),
                          pltpu.VMEM((inner, part, n), F32), pltpu.VMEM((inner, heads, n), F32),
                          pltpu.VMEM((part, n), F32), pltpu.VMEM((part, n), F32),
                          pltpu.VMEM((inner, part, n), F32), pltpu.VMEM((inner, part, n), F32)] + sems,
        compiler_params=pltpu.CompilerParams(dimension_semantics=("arbitrary",), collective_id=0,
                                             has_side_effects=True, vmem_limit_bytes=60 << 20),
        name="outputs",
    )(x, gate, w, e, reach, input_proj, output_proj, loc, last, logs, norm_gain.reshape(rows, 1))
    return jnp.transpose(result.reshape(heads, width, tokens), (2, 0, 1))


def solution(mesh):
    in_specs = (P("ctx", "grp", None), P("ctx", "grp", None), P("ctx", "grp"), P("grp"), P("grp"),
                P("ctx", None), P("ctx", None), P("grp", None))
    return jax.shard_map(shards, mesh=mesh, in_specs=in_specs, out_specs=P("ctx", "grp", None), check_vma=False)
```

time: 97.1 us -> 83.3 us (0.86); the launches traced: 95.3 us -> 82.6 us
  other arithmetic: 12.8 us -> 0.68 us
  local copies, waits for them, and re-layouts: 5.83 us -> 14.1 us
  Pallas kernels: 72.3 us -> 67.8 us
  blocking collectives: 4.31 us -> 0 us
    convert_element_type x1 -> x0, other arithmetic: 12.8 us -> none  [shards(): result = (gated * scale * norm_gain.reshape(rows, 1)).astype(BF16)]
    unnamed x8 -> x1, local copies, waits for them, and re-layouts: 3.09 us -> 10.3 us
    psum x1 -> x0, blocking collectives: 4.31 us -> none  [shards(): total_sq = lax.psum(local_sq, 'grp')]
    pallas_call x2 -> x1, Pallas kernels: 57.5 us -> 54.2 us  [shards(): pl.pallas_call(functools.partial(output_kernel, count, others, inner, pie...]
    reshape x0 -> x1, local copies, waits for them, and re-layouts: none -> 3.12 us  [shards(): norm_gain.reshape(rows, 1)]
    broadcast_in_dim x2 -> x0, local copies, waits for them, and re-layouts: 2.67 us -> none  [shards(): bias, rate = (step_bias[:, None], decay_rate[:, None])]
    pallas_call x1, Pallas kernels: 14.7 us -> 13.6 us  [shards(): pl.pallas_call(functools.partial(state_kernel, heads, width, group), grid...]
where the time goes in v3:
time: 83.3 us; the launch traced here: 82.6 us
  Pallas kernels  67.8 us (81%)
  local copies, waits for them, and re-layouts  14.1 us (17%)
    pallas_call x1, Pallas kernels, shards(): pl.pallas_call(functools.partial(output_kernel, count, others, inner, pie...  54.2 us
    pallas_call x1, Pallas kernels, shards(): pl.pallas_call(functools.partial(state_kernel, heads, width, group), grid...  13.6 us
    unnamed x1, local copies, waits for them, and re-layouts  10.3 us
    reshape x1, local copies, waits for them, and re-layouts, shards(): norm_gain.reshape(rows, 1)  3.12 us

profile of v3, /device:TPU:25, one launch (start us, length us, event | category | flops | bytes accessed | tf_op | source)
XLA Modules:
  0.0 82.6 jit_solution(18333855588149893541)
XLA Ops:
  0.0 0.7 pad_maximum_fusion
  0.7 0.7 copy.14.head_ref
  1.4 3.1 %reshape.16.gain_ref = f32[2560,1]{1,0:T(8,128)} reshape(f32[40,64]{1,0:T(8,128)} %param.15) | data formatting | bytes 20480 | tf_op jit(solution)/shard_map/reshape | solution.py:346
  4.5 13.6 %local_state.1 = (f32[8,2560,128]{2,1,0:T(8,128)}, f32[2560,128]{1,0:T(8,128)}, f32[40,128]{1,0:T(8,128)}, f32[40,2048]{1,0:T(8,128)}, f32[40,2048]{1,0:T(8,128)}, /*index=5*/f32[40,2048]{1,0:T(8,128)}) custom-call(bf16[2560,2048]{1,0:T(8,128)(2,1)} %bitcast.12, f32[40,2048]{1,0:T(8,128)} %bitcast.16, f32[40,2]{1,0:T(8,128)} %copy.14.head_ref, ...), custom_call_target="tpu_custom_call" | custom-call | tf_op jit(solution)/shard_map/local_state/pallas_call | solution.py:297
  18.1 54.2 %outputs.1 = bf16[2560,2048]{1,0:T(8,128)(2,1)} custom-call(bf16[2560,2048]{1,0:T(8,128)(2,1)} %bitcast.13, bf16[2560,2048]{1,0:T(8,128)(2,1)} %bitcast.15, f32[40,2048]{1,0:T(8,128)} %get-tuple-element.11.w_ref, f32[40,2048]{1,0:T(8,128)} %get-tuple-element.12.e_ref, f32[40,2048]{1,0:T(8,128)} %get-tuple-element.13.reach_ref, bf16[2048,128]{1,0:T(8,128)(2,1)} %b_ref.3, ...), custom_call_target="tpu_custom_call" | custom-call | tf_op jit(solution)/shard_map/outputs/pallas_call | solution.py:322
  72.3 10.3 %copy.17 = bf16[2048,40,64]{0,2,1:T(8,128)(2,1)} copy(bf16[2048,40,64]{0,2,1:T(8,128)(2,1)} %bitcast.14) | data formatting | bytes 20971520
